TPU v7x, 32 devices: a whole 2x2x4 slice. The times are simulated.
32 devices in a mesh: seq: 8 (over z, core), tp: 4 (over y, x).
Axes of the slice: x: 2, y: 2, z: 4, core: 2. Of those that a mesh axis runs over, the one named last changes fastest.
Arguments:
- hidden_in: bfloat16 [4096, 4608], P('seq'), may hold values from -6 to 6
- pre_gain: float32 [4608], replicated, may hold values from 0.5 to 1.5
- w_query: bfloat16 [4608, 4096], P(None, 'tp'), may hold values from -0.09375 to 0.09375
- key_cache: bfloat16 [8192, 2048], P('seq', 'tp'), may hold values from -12 to 12
- value_cache: bfloat16 [8192, 2048], P('seq', 'tp'), may hold values from -6 to 6
- w_out: bfloat16 [4096, 4608], P('tp'), may hold values from -0.75 to 0.75
- post_gain: float32 [4608], replicated, may hold values from 0.5 to 1.5
- starts: int32 [8], replicated, may hold values from 0 to 7680, as said below
- counts: int32 [8], replicated, may hold values from 512 to 1024, as said below
Outputs:
- layer_out: bfloat16 [4096, 4608], P(('seq', 'tp'))
Inputs may be any that keep to these rules, and one draw needn't show every extreme that they name: The queries of shard s sit at positions starts[s] to starts[s] + 511, all inside the filled rows of shard s, that is from s * 1024 to s * 1024 + counts[s] - 1. `counts`: at least one shard is full.
All inputs are finite; a program needn't handle non-finite values.
Results may differ from a plain program's by a relative error of at most 0.012.
Values may be sent and summed in bfloat16 or wider, within the bound.
A program may use at most 128 MiB of HBM per device.

v0:
```python
import functools
import math

import jax
import jax.numpy as jnp
from jax import lax
from jax.experimental import pallas as pl
from jax.experimental.pallas import tpu as pltpu
from jax.sharding import PartitionSpec as P

HEADS = 32
HD = 128
WINDOW = 4096
SUB = 16
QT = 256
NT = 256
SOFT = 50.0
GAIN = SOFT * math.log2(math.e)
MESH = pl.DeviceIdType.MESH
F32 = jnp.float32
BF16 = jnp.bfloat16


def kernel(
    n, n_tp, kvh, NC,
    starts, counts, hidden, pre_gain, wq, key, value, wout, post_gain, out,
    hbuf, wqb, wob, k0, v0, k2, v2, k1, v1, qo, qr, vx0, vx1, vx2, ao, ar, psend, precv,
    proj, ra1, pa, ra2, rb1, pb, rb2, res, obuf, att,
    hsem, wqsem, wosem, kvsem, ressem, osem,
    s2, r2, s1, r1, sq, rq, sp, rp,
    sa1, ta1, sa2, ta2, sb1, tb1, sb2, tb2,
):
    s = lax.axis_index("seq")
    t = lax.axis_index("tp")
    odd = lax.rem(s, 2)
    partner = s + 1 - 2 * odd
    rows, d = hidden.shape
    ctx = key.shape[0]
    sub = rows // (NC * n_tp)
    chunk = rows // NC
    owned = rows // n_tp
    has_prev = s >= 2
    has_next = s + 2 < n

    hcopies = []
    for c in range(NC):
        for b in range(n_tp):
            cp = pltpu.make_async_copy(
                hidden.at[pl.ds(b * owned + c * sub, sub)], hbuf.at[c, b], hsem.at[c, b])
            cp.start()
            hcopies.append(cp)

    def wq_copy(h):
        return pltpu.make_async_copy(
            wq.at[:, pl.ds(pl.multiple_of(h * 2 * HD, 2 * HD), 2 * HD)], wqb.at[h], wqsem.at[h])

    for h in range(kvh):
        wq_copy(h).start()

    barrier = pltpu.get_barrier_semaphore()
    pl.semaphore_signal(barrier, inc=1, device_id=(partner, t), device_id_type=MESH)
    for k in range(1, n_tp):
        pl.semaphore_signal(barrier, inc=1, device_id=(s, lax.rem(t + k, n_tp)), device_id_type=MESH)

    @pl.when(has_prev)
    def _():
        pl.semaphore_signal(barrier, inc=1, device_id=(s - 2, t), device_id_type=MESH)

    @pl.when(has_next)
    def _():
        pl.semaphore_signal(barrier, inc=1, device_id=(s + 2, t), device_id_type=MESH)

    pl.semaphore_wait(
        barrier, n_tp + jnp.where(has_prev, 1, 0) + jnp.where(has_next, 1, 0))

    def cols(h):
        return pl.ds(pl.multiple_of(h * HD, HD), HD)

    def kv_next(h):
        return [
            pltpu.make_async_remote_copy(
                src.at[:, cols(h)], dst.at[h], s2.at[h, j], r2.at[h, j],
                device_id=(s + 2, t), device_id_type=MESH)
            for j, (src, dst) in enumerate(((key, k2), (value, v2)))
        ]

    def kv_own_partner(h):
        return [
            pltpu.make_async_remote_copy(
                src.at[:, cols(h)], dst.at[h], s1.at[h, j], r1.at[h, j],
                device_id=(partner, t), device_id_type=MESH)
            for j, (src, dst) in enumerate(((key, k1), (value, v1)))
        ]

    def kv_relay(h):
        return [
            pltpu.make_async_remote_copy(
                src.at[h], dst.at[h], s1.at[h, j], r1.at[h, j],
                device_id=(partner, t), device_id_type=MESH)
            for j, (src, dst) in enumerate(((k2, k1), (v2, v1)))
        ]

    def q_back(h):
        return pltpu.make_async_remote_copy(
            qo.at[h], qr.at[h], sq.at[h], rq.at[h], device_id=(s - 2, t), device_id_type=MESH)

    def part_next(c):
        return pltpu.make_async_remote_copy(
            psend.at[c], precv.at[c], sp.at[c], rp.at[c],
            device_id=(s + 2, t), device_id_type=MESH)

    nx = 2
    ny = n_tp // nx
    half = d // 2
    x_own = lax.rem(t, nx)
    y_own = lax.div(t, nx)
    left = pl.ds(0, half)
    right = pl.ds(half, half)

    def remote(src, dst, send, recv, to):
        return pltpu.make_async_remote_copy(
            src, dst, send, recv, device_id=(s, to), device_id_type=MESH)

    def first_phase(c):
        copies = []
        for k in range(1, nx):
            xt = lax.rem(x_own + k, nx)
            copies.append(remote(
                proj.at[c, :, xt, :, left], ra1.at[c, k - 1], sa1.at[c, k - 1], ta1.at[c, k - 1],
                y_own * nx + xt))
        for k in range(1, ny):
            yt = lax.rem(y_own + k, ny)
            copies.append(remote(
                proj.at[c, yt, :, :, right], rb1.at[c, k - 1], sb1.at[c, k - 1], tb1.at[c, k - 1],
                yt * nx + x_own))
        return copies

    def second_phase(c):
        copies = []
        for k in range(1, ny):
            yt = lax.rem(y_own + k, ny)
            copies.append(remote(
                pa.at[c, yt], ra2.at[c, k - 1], sa2.at[c, k - 1], ta2.at[c, k - 1],
                yt * nx + x_own))
        for k in range(1, nx):
            xt = lax.rem(x_own + k, nx)
            copies.append(remote(
                pb.at[c, xt], rb2.at[c, k - 1], sb2.at[c, k - 1], tb2.at[c, k - 1],
                y_own * nx + xt))
        return copies

    @pl.when(has_next)
    def _():
        for h in range(kvh):
            for cp in kv_next(h):
                cp.start()

    @pl.when(odd == 0)
    def _():
        for h in range(kvh):
            for cp in kv_own_partner(h):
                cp.start()

    def kv_local(h):
        return [
            pltpu.make_async_copy(src.at[:, cols(h)], dst.at[h], kvsem.at[h, j])
            for j, (src, dst) in enumerate(((key, k0), (value, v0)))
        ]

    for h in range(kvh):
        for cp in kv_local(h):
            cp.start()
    wo_copy = pltpu.make_async_copy(wout, wob, wosem)
    wo_copy.start()
    res_copy = pltpu.make_async_copy(
        hidden.at[pl.ds(pl.multiple_of(t * owned, owned), owned)], res, ressem)
    res_copy.start()

    for cp in hcopies:
        cp.wait()

    def norm(i, carry):
        c = i // n_tp
        b = i % n_tp
        x = hbuf[c, b].astype(F32)
        y = x * lax.rsqrt(jnp.mean(x * x, axis=-1, keepdims=True) + 0.1) * pre_gain[...]
        hbuf[c, b] = y.astype(BF16)
        return carry

    lax.fori_loop(0, NC * n_tp, norm, 0)

    def project(h, carry):
        wq_copy(h).wait()
        x = hbuf[...].reshape(rows, d)
        y = jnp.dot(x, wqb[h], preferred_element_type=F32) * ((d // HEADS) ** -0.5 / SOFT)
        y = y.astype(BF16)
        qo[h, 0:rows] = y[:, :HD]
        qo[h, rows:2 * rows] = y[:, HD:]

        @pl.when(has_prev)
        def _():
            q_back(h).start()

        return carry

    lax.fori_loop(0, kvh, project, 0)

    def extend(vx, v, h, filled):
        r = lax.broadcasted_iota(jnp.int32, (ctx, HD), 0)
        ok = r < filled
        vx[:, 0:HD] = jnp.where(ok, v[h].astype(F32), 0.0).astype(BF16)
        vx[:, HD:] = jnp.where(ok, 1.0, 0.0).astype(BF16)

    def unit(q, k, vx, h, acc, first, mode, offset):
        per = QT // chunk

        def tile(i, carry):
            span = pl.ds(pl.multiple_of(i * QT, QT), QT)
            qt = q[h, span]
            ps = []
            kb = 256
            if mode:
                shape = (per, n_tp, sub, kb)
                c0 = lax.rem(i * per, NC)
                pos = (
                    (c0 + lax.broadcasted_iota(jnp.int32, shape, 0)) * sub
                    + lax.broadcasted_iota(jnp.int32, shape, 1) * owned
                    + lax.broadcasted_iota(jnp.int32, shape, 2)
                )
                rel = (lax.broadcasted_iota(jnp.int32, shape, 3) - pos - offset).reshape(QT, kb)
            for b in range(ctx // kb):
                sc = lax.dot_general(
                    qt, k[h, b * kb:(b + 1) * kb], (((1,), (1,)), ((), ())),
                    preferred_element_type=F32)
                p = jnp.exp2(jnp.tanh(sc) * GAIN)
                if mode == 1:
                    p = jnp.where(rel <= -b * kb, p, 0.0)
                elif mode == 2:
                    p = jnp.where(rel > -b * kb, p, 0.0)
                ps.append(p.astype(BF16))
            a = jnp.dot(jnp.concatenate(ps, axis=1), vx[...], preferred_element_type=F32)
            if first:
                acc[h, span] = a
            else:
                acc[h, span] += a
            return carry

        lax.fori_loop(0, 2 * rows // QT, tile, 0, unroll=2)

    off_own = starts[s] - s * ctx
    s_next = jnp.minimum(s + 2, n - 1)
    off_next = starts[s_next] - s_next * ctx + (2 + 2) * ctx - WINDOW
    fill1 = counts[jnp.maximum(s - 1, 0)]
    fill2 = counts[jnp.maximum(s - 2, 0)]

    def own(h):
        for cp in kv_local(h):
            cp.wait()
        extend(vx0, v0, h, ctx)
        unit(qo, k0, vx0, h, ao, True, 1, off_own)

    def back(h):
        @pl.when(has_prev)
        def _():
            for cp in kv_next(h):
                cp.wait_recv()

        @pl.when(has_prev & (odd == 1))
        def _():
            for cp in kv_relay(h):
                cp.start()

        @pl.when(has_next)
        def _():
            q_back(h).wait_recv()
            ar[h] = jnp.zeros_like(ar[h])

        @pl.when(has_prev)
        def _():
            extend(vx2, v2, h, fill2)

            @pl.when(has_next)
            def _():
                unit(qr, k2, vx2, h, ar, False, 2, off_next)

        @pl.when(s >= 1)
        def _():
            for cp in kv_own_partner(h):
                cp.wait_recv()

            extend(vx1, v1, h, fill1)

            @pl.when(has_next)
            def _():
                unit(qr, k1, vx1, h, ar, False, 0, 0)

    def far(h):
        @pl.when(has_prev)
        def _():
            unit(qo, k2, vx2, h, ao, False, 0, 0)

        @pl.when(s >= 1)
        def _():
            unit(qo, k1, vx1, h, ao, False, 0, 0)

    own(0)

    def head(h, carry):
        back(h)

        @pl.when(h < kvh - 1)
        def _():
            far(h)
            own(h + 1)

        return carry

    lax.fori_loop(0, kvh, head, 0)

    lane = lax.broadcasted_iota(jnp.int32, (chunk, HD), 1)
    heads = 2 * kvh

    @pl.when(has_next)
    def _():
        for c in range(NC):
            pack = jnp.zeros((chunk, HD), F32)
            for h in range(kvh):
                for g in range(2):
                    r0 = g * rows + c * chunk
                    j = 2 * h + g
                    psend[c, j] = ar[h, r0:r0 + chunk, 0:HD].astype(BF16)
                    den = ar[h, r0:r0 + chunk, HD:2 * HD]
                    hi = den.astype(BF16).astype(F32)
                    pack = jnp.where(lane == j, hi, pack)
                    pack = jnp.where(lane == heads + j, den - hi, pack)
            psend[c, heads] = pack.astype(BF16)
            part_next(c).start()

    far(kvh - 1)
    wo_copy.wait()

    @pl.when(s < 2)
    def _():
        precv[...] = jnp.zeros_like(precv)

    def finish(c, carry):
        @pl.when(has_prev)
        def _():
            part_next(c).wait_recv()

        pack = precv[c, heads].astype(F32)
        for h in range(kvh):
            for g in range(2):
                j = 2 * h + g
                span = pl.ds(pl.multiple_of(g * rows + c * chunk, chunk), chunk)
                den = (
                    ao[h, span, HD:2 * HD]
                    + pack[:, j:j + 1] + pack[:, heads + j:heads + j + 1]
                )
                num = ao[h, span, 0:HD] + precv[c, j].astype(F32)
                att[:, j * HD:(j + 1) * HD] = (num / den).astype(BF16)

        def column(i, inner):
            cs = pl.ds(pl.multiple_of(i * NT, NT), NT)
            y = jnp.dot(att[...], wob[:, cs], preferred_element_type=F32).astype(BF16)
            proj[c, :, :, :, cs] = y.reshape(ny, nx, sub, NT)
            return inner

        lax.fori_loop(0, d // NT, column, 0)
        for cp in first_phase(c):
            cp.start()

        @pl.when(c >= 1)
        def _():
            middle(c - 1)

        return carry

    def middle(c):
        for cp in first_phase(c):
            cp.wait_recv()
        for y in range(ny):
            part = proj[c, y, x_own, :, 0:half].astype(F32)
            for k in range(1, nx):
                part += ra1[c, k - 1, y].astype(F32)
            pa[c, y] = part.astype(BF16)
        for x in range(nx):
            part = proj[c, y_own, x, :, half:d].astype(F32)
            for k in range(1, ny):
                part += rb1[c, k - 1, x].astype(F32)
            pb[c, x] = part.astype(BF16)
        for cp in second_phase(c):
            cp.start()

    lax.fori_loop(0, NC, finish, 0)
    middle(NC - 1)
    res_copy.wait()

    def out_copy(c):
        return pltpu.make_async_copy(
            obuf.at[c], out.at[pl.ds(pl.multiple_of(c * sub, sub), sub)], osem.at[c])

    def close(c, carry):
        for cp in second_phase(c):
            cp.wait_recv()
        lo = pa[c, y_own].astype(F32)
        for k in range(1, ny):
            lo += ra2[c, k - 1].astype(F32)
        hi = pb[c, x_own].astype(F32)
        for k in range(1, nx):
            hi += rb2[c, k - 1].astype(F32)
        squares = jnp.sum(lo * lo, axis=-1, keepdims=True) + jnp.sum(hi * hi, axis=-1, keepdims=True)
        scale = lax.rsqrt(squares / d + 0.1)
        span = pl.ds(pl.multiple_of(c * sub, sub), sub)
        for v, at in ((lo, slice(0, half)), (hi, slice(half, d))):
            r = res[span, at].astype(F32)
            obuf[c, :, at] = (r + v * scale * post_gain[:, at]).astype(BF16)
        out_copy(c).start()
        return carry

    lax.fori_loop(0, NC, close, 0)

    def drain(h, carry):
        @pl.when(has_next)
        def _():
            for cp in kv_next(h):
                cp.wait_send()

        @pl.when(odd == 0)
        def _():
            for cp in kv_own_partner(h):
                cp.wait_send()

        @pl.when(has_prev & (odd == 1))
        def _():
            for cp in kv_relay(h):
                cp.wait_send()

        @pl.when(has_prev)
        def _():
            q_back(h).wait_send()

        return carry

    lax.fori_loop(0, kvh, drain, 0)

    def drain_chunks(c, carry):
        @pl.when(has_next)
        def _():
            part_next(c).wait_send()

        for cp in first_phase(c) + second_phase(c):
            cp.wait_send()
        out_copy(c).wait()
        return carry

    lax.fori_loop(0, NC, drain_chunks, 0)


def shards(n, n_tp, hidden_in, pre_gain, w_query, key_cache, value_cache, w_out, post_gain, starts, counts):
    rows, d = hidden_in.shape
    ctx, kvw = key_cache.shape
    kvh = kvw // HD
    sub = SUB
    NC = rows // (n_tp * sub)
    chunk = rows // NC
    nx, ny, half = 2, n_tp // 2, d // 2
    dma = pltpu.SemaphoreType.DMA
    kv = pltpu.VMEM((kvh, ctx, HD), BF16)
    any_spec = pl.BlockSpec(memory_space=pl.ANY)
    vmem_spec = pl.BlockSpec(memory_space=pltpu.VMEM)
    smem_spec = pl.BlockSpec(memory_space=pltpu.SMEM)
    return pl.pallas_call(
        functools.partial(kernel, n, n_tp, kvh, NC),
        out_shape=jax.ShapeDtypeStruct((rows // n_tp, d), BF16),
        in_specs=[smem_spec, smem_spec, any_spec, vmem_spec] + [any_spec] * 4 + [vmem_spec],
        out_specs=any_spec,
        scratch_shapes=[
            pltpu.VMEM((NC, n_tp, sub, d), BF16),
            pltpu.VMEM((kvh, d, 2 * HD), BF16),
            pltpu.VMEM(w_out.shape, BF16),
            kv, kv, kv, kv, kv, kv,
            pltpu.VMEM((kvh, 2 * rows, HD), BF16),
            pltpu.VMEM((kvh, 2 * rows, HD), BF16),
            pltpu.VMEM((ctx, 2 * HD), BF16),
            pltpu.VMEM((ctx, 2 * HD), BF16),
            pltpu.VMEM((ctx, 2 * HD), BF16),
            pltpu.VMEM((kvh, 2 * rows, 2 * HD), F32),
            pltpu.VMEM((kvh, 2 * rows, 2 * HD), F32),
            pltpu.VMEM((NC, 2 * kvh + 1, chunk, HD), BF16),
            pltpu.VMEM((NC, 2 * kvh + 1, chunk, HD), BF16),
            pltpu.VMEM((NC, ny, nx, sub, d), BF16),
            pltpu.VMEM((NC, nx - 1, ny, sub, half), BF16),
            pltpu.VMEM((NC, ny, sub, half), BF16),
            pltpu.VMEM((NC, ny - 1, sub, half), BF16),
            pltpu.VMEM((NC, ny - 1, nx, sub, half), BF16),
            pltpu.VMEM((NC, nx, sub, half), BF16),
            pltpu.VMEM((NC, nx - 1, sub, half), BF16),
            pltpu.VMEM((rows // n_tp, d), BF16),
            pltpu.VMEM((NC, sub, d), BF16),
            pltpu.VMEM((chunk, w_out.shape[0]), BF16),
            dma((NC, n_tp)), dma((kvh,)), dma, dma((kvh, 2)), dma, dma((NC,)),
            dma((kvh, 2)), dma((kvh, 2)), dma((kvh, 2)), dma((kvh, 2)),
            dma((kvh,)), dma((kvh,)), dma((NC,)), dma((NC,)),
            dma((NC, nx - 1)), dma((NC, nx - 1)), dma((NC, ny - 1)), dma((NC, ny - 1)),
            dma((NC, ny - 1)), dma((NC, ny - 1)), dma((NC, nx - 1)), dma((NC, nx - 1)),
        ],
        compiler_params=pltpu.CompilerParams(
            collective_id=0, has_side_effects=True, vmem_limit_bytes=67_000_000),
        name="attention_block",
    )(starts, counts, hidden_in, pre_gain.reshape(1, d), w_query, key_cache, value_cache, w_out,
      post_gain.reshape(1, d))


def solution(mesh):
    return jax.shard_map(
        functools.partial(shards, mesh.shape["seq"], mesh.shape["tp"]),
        mesh=mesh,
        in_specs=(
            P("seq", None),
            P(),
            P(None, "tp"),
            P("seq", "tp"),
            P("seq", "tp"),
            P("tp", None),
            P(),
            P(),
            P(),
        ),
        out_specs=P(("seq", "tp"), None),
        check_vma=False,
    )
```

profile of v0, /device:TPU:16, one launch (start us, length us, event | category | flops | bytes accessed | tf_op | source)
XLA Modules:
  0.0 112.1 jit_solution(13422266192498942079)
XLA Ops:
  0.0 1.3 %reshape.6.pre_gain = f32[1,4608]{1,0:T(1,128)} reshape(f32[4608]{0:T(1024)} %param.10) | data formatting | bytes 36864 | tf_op jit(solution)/shard_map/reshape | solution.py:511
  1.3 1.3 %reshape.7.post_gain = f32[1,4608]{1,0:T(1,128)} reshape(f32[4608]{0:T(1024)} %param.15) | data formatting | bytes 36864 | tf_op jit(solution)/shard_map/reshape | solution.py:512
  2.7 107.0 %attention_block.1 = bf16[128,4608]{1,0:T(8,128)(2,1)} custom-call(s32[8]{0:T(128)} %starts.1, s32[8]{0:T(128)} %counts.1, bf16[512,4608]{1,0:T(8,128)(2,1)} %hidden.1, f32[1,4608]{1,0:T(1,128)} %reshape.6.pre_gain, bf16[4608,1024]{1,0:T(8,128)(2,1)} %wq.1, bf16[1024,512]{1,0:T(8,128)(2,1)} %key.1, bf16[1024,512]{1,0:T(8,128)(2,1)} %value.1, ...), custom_call_target="tpu_custom_call" | custom-call | tf_op jit(solution)/shard_map/attention_block/pallas_call | solution.py:473
  109.7 2.4 %copy.11 = bf16[128,4608]{1,0:T(8,128)(2,1)} copy(bf16[128,4608]{1,0:T(8,128)(2,1)} %attention_block.1) | data formatting | bytes 2359296
where the time goes:
time: 112 us
  Pallas kernels  107 us (96%)
  local copies, waits for them, and re-layouts  5.04 us (4%)
    pallas_call x1, Pallas kernels, shards(): pl.pallas_call(functools.partial(kernel, n, n_tp, kvh, NC), out_shape=jax...  107 us
    unnamed x1, local copies, waits for them, and re-layouts  2.36 us

commit v1 on v0

v1 whole, which is shorter than its diff:
```python
import functools
import math

import jax
import jax.numpy as jnp
from jax import lax
from jax.experimental import pallas as pl
from jax.experimental.pallas import tpu as pltpu
from jax.sharding import PartitionSpec as P

HEADS = 32
HD = 128
WINDOW = 4096
SUB = 16
G = 2
KB = 256
KT = 512
NT = 2304
SOFT = 50.0
GAIN = SOFT * math.log2(math.e)
MESH = pl.DeviceIdType.MESH
F32 = jnp.float32
BF16 = jnp.bfloat16


def kernel(
    n, n_tp, kvh, NC,
    starts, counts, hidden, pre_gain, wq, key, value, wout, post_gain, out,
    hbuf, wqb, wob, kraw, kt, vb, q0, q2, q4, fs, fr, ns, nr, acc, accd, num, den, rel, sc0, sc1, pw0, pw1,
    proj, ra1, pa, ra2, rb1, pb, rb2, res, obuf, att,
    hsem, wqsem, wosem, kvsem, ressem, osem,
    s1, r1, sn, rn, sf, rf, sF, rF, sN, rN,
    sa1, ta1, sa2, ta2, sb1, tb1, sb2, tb2,
):
    sc = (sc0, sc1)
    pw = (pw0, pw1)
    s = lax.axis_index("seq")
    t = lax.axis_index("tp")
    odd = lax.rem(s, 2)
    partner = s + 1 - 2 * odd
    rows, d = hidden.shape
    ctx = key.shape[0]
    sub = rows // (NC * n_tp)
    chunk = rows // NC
    tall = 2 * chunk
    owned = rows // n_tp
    NF = NC // G
    has_prev = s >= 2
    has_next = s + 2 < n
    has_far = s + 4 < n

    def h_copy(c, b):
        return pltpu.make_async_copy(
            hidden.at[pl.ds(pl.multiple_of(b * owned + c * sub, sub), sub)], hbuf.at[c, b], hsem.at[c, b])

    def wq_copy(h):
        return pltpu.make_async_copy(
            wq.at[:, pl.ds(pl.multiple_of(h * 2 * HD, 2 * HD), 2 * HD)], wqb.at[h], wqsem.at[h])

    def cols(h):
        return pl.ds(pl.multiple_of(h * HD, HD), HD)

    def kv_local(h):
        return [
            pltpu.make_async_copy(src.at[:, cols(h)], dst.at[0, h], kvsem.at[h, j])
            for j, (src, dst) in enumerate(((key, kraw), (value, vb)))
        ]

    for c in range(NC // 2):
        for b in range(n_tp):
            h_copy(c, b).start()
    for h in range(kvh):
        wq_copy(h).start()
    for c in range(NC // 2, NC):
        for b in range(n_tp):
            h_copy(c, b).start()
    for h in range(kvh):
        for cp in kv_local(h):
            cp.start()

    barrier = pltpu.get_barrier_semaphore()
    pl.semaphore_signal(barrier, inc=1, device_id=(partner, t), device_id_type=MESH)
    for k in range(1, n_tp):
        pl.semaphore_signal(barrier, inc=1, device_id=(s, lax.rem(t + k, n_tp)), device_id_type=MESH)

    @pl.when(has_prev)
    def _():
        pl.semaphore_signal(barrier, inc=1, device_id=(s - 2, t), device_id_type=MESH)

    @pl.when(has_next)
    def _():
        pl.semaphore_signal(barrier, inc=1, device_id=(s + 2, t), device_id_type=MESH)

    pl.semaphore_wait(
        barrier, n_tp + jnp.where(has_prev, 1, 0) + jnp.where(has_next, 1, 0))

    def kv_partner(h):
        return [
            pltpu.make_async_remote_copy(
                src.at[:, cols(h)], dst.at[1, h], s1.at[h, j], r1.at[h, j],
                device_id=(partner, t), device_id_type=MESH)
            for j, (src, dst) in enumerate(((key, kraw), (value, vb)))
        ]

    def along(src, dst, send, recv, to):
        def make(c):
            return pltpu.make_async_remote_copy(
                src.at[c], dst.at[c], send.at[c], recv.at[c],
                device_id=(to, t), device_id_type=MESH)
        return make

    q_near = along(q0, q2, sn, rn, s - 2)
    q_far = along(q2, q4, sf, rf, s - 2)
    p_far = along(fs, fr, sF, rF, s + 2)
    p_near = along(ns, nr, sN, rN, s + 2)

    nx = 2
    ny = n_tp // nx
    half = d // 2
    x_own = lax.rem(t, nx)
    y_own = lax.div(t, nx)
    left = pl.ds(0, half)
    right = pl.ds(half, half)

    def remote(src, dst, send, recv, to):
        return pltpu.make_async_remote_copy(
            src, dst, send, recv, device_id=(s, to), device_id_type=MESH)

    def first_phase(c):
        copies = []
        for k in range(1, nx):
            xt = lax.rem(x_own + k, nx)
            copies.append(remote(
                proj.at[c, :, xt, :, :, left], ra1.at[c, k - 1], sa1.at[c, k - 1], ta1.at[c, k - 1],
                y_own * nx + xt))
        for k in range(1, ny):
            yt = lax.rem(y_own + k, ny)
            copies.append(remote(
                proj.at[c, yt, :, :, :, right], rb1.at[c, k - 1], sb1.at[c, k - 1], tb1.at[c, k - 1],
                yt * nx + x_own))
        return copies

    def second_phase(c):
        copies = []
        for k in range(1, ny):
            yt = lax.rem(y_own + k, ny)
            copies.append(remote(
                pa.at[c, yt], ra2.at[c, k - 1], sa2.at[c, k - 1], ta2.at[c, k - 1],
                yt * nx + x_own))
        for k in range(1, nx):
            xt = lax.rem(x_own + k, nx)
            copies.append(remote(
                pb.at[c, xt], rb2.at[c, k - 1], sb2.at[c, k - 1], tb2.at[c, k - 1],
                y_own * nx + xt))
        return copies

    for h in range(kvh):
        for cp in kv_partner(h):
            cp.start()
    wo_copy = pltpu.make_async_copy(wout, wob, wosem)
    wo_copy.start()
    res_copy = pltpu.make_async_copy(
        hidden.at[pl.ds(pl.multiple_of(t * owned, owned), owned)], res, ressem)
    res_copy.start()

    shape = (2, n_tp, sub, KB)
    rel[...] = (
        lax.broadcasted_iota(jnp.int32, shape, 3)
        - lax.broadcasted_iota(jnp.int32, shape, 1) * owned
        - lax.broadcasted_iota(jnp.int32, shape, 2)
    ).reshape(tall, KB)

    @pl.when(s < 2)
    def _():
        fr[...] = jnp.zeros_like(fr)
        nr[...] = jnp.zeros_like(nr)

    def queries(c0, count):
        def norm(i, carry):
            c = c0 + i // n_tp
            b = i % n_tp
            h_copy(c, b).wait()
            x = hbuf[c, b].astype(F32)
            y = x * lax.rsqrt(jnp.mean(x * x, axis=-1, keepdims=True) + 0.1) * pre_gain[...]
            hbuf[c, b] = y.astype(BF16)
            return carry

        lax.fori_loop(0, count * n_tp, norm, 0, unroll=4)

        def project(h, carry):
            if c0 == 0:
                wq_copy(h).wait()
            x = hbuf[c0:c0 + count].reshape(count * chunk, d)
            y = jnp.dot(x, wqb[h], preferred_element_type=F32) * ((d // HEADS) ** -0.5 / SOFT)
            y = y.astype(BF16)
            for i in range(count):
                q0[c0 + i, h, 0:chunk] = y[i * chunk:(i + 1) * chunk, :HD]
                q0[c0 + i, h, chunk:tall] = y[i * chunk:(i + 1) * chunk, HD:]
            return carry

        lax.fori_loop(0, kvh, project, 0)

    queries(0, NC // 2)

    @pl.when(has_prev)
    def _():
        q_near(0).start()
        q_near(1).start()

    queries(NC // 2, NC // 2)

    def turn(src):
        def body(h, carry):
            for cp in (kv_local(h) if src == 0 else kv_partner(h)):
                if src == 0:
                    cp.wait()
                else:
                    cp.wait_recv()
            kt[src, h] = kraw[src, h].T
            return carry

        lax.fori_loop(0, kvh, body, 0)

    turn(0)
    turn(1)

    off_own = starts[s] - s * ctx
    s_far = jnp.minimum(s + 4, n - 1)
    off_far = starts[s_far] - s_far * ctx + 4 * ctx - WINDOW
    fill0 = counts[s]
    fill1 = counts[partner]
    lane = lax.broadcasted_iota(jnp.int32, (1, KB), 1)

    def unit(q, c, sources, num, den):
        tiles = [
            (h, src, mode, i)
            for h in range(kvh) for src, mode in sources for i in range(ctx // KT)
        ]
        last = len(sources) * (ctx // KT)
        tops = {}
        belows = {}

        def scores(j):
            h, src, mode, i = tiles[j]
            qt = q[c, h]
            for b in range(0, KT, KB):
                at = i * KT + b
                sc[j % 2][:, b:b + KB] = jnp.dot(
                    qt, kt[src, h, :, at:at + KB], preferred_element_type=F32)

        def weights(j):
            h, src, mode, i = tiles[j]
            fill = fill1 if src else fill0
            below = belows.get(h)
            for b in range(0, KT, KB):
                at = i * KT + b
                p = jnp.exp2(jnp.tanh(sc[j % 2][:, b:b + KB]) * GAIN)
                if mode == 1:
                    p = jnp.where(rel[...] <= off_own + c * sub - at, p, 0.0)
                elif mode == 2:
                    ok = (rel[...] > off_far + c * sub - at) & (lane < fill - at)
                    p = jnp.where(ok, p, 0.0)
                else:
                    p = jnp.where(lane < fill - at, p, 0.0)
                for k in range(0, KB, HD):
                    part = p[:, k:k + HD]
                    below = part if below is None else below + part
                pw[j % 2][:, b:b + KB] = p.astype(BF16)
            belows[h] = below
            if j % last == last - 1:
                den[h] = below

        def values(j):
            h, src, mode, i = tiles[j]
            a = jnp.dot(
                pw[j % 2][...], vb[src, h, i * KT:(i + 1) * KT], preferred_element_type=F32)
            tops[h] = tops[h] + a if h in tops else a
            if j % last == last - 1:
                num[h] = tops[h]

        count = len(tiles)
        for k in range(count + 2):
            if k < count:
                scores(k)
            if 0 <= k - 1 < count:
                weights(k - 1)
            if 0 <= k - 2:
                values(k - 2)

    blocks = tall // HD
    lanes = lax.broadcasted_iota(jnp.int32, (tall, HD), 1)

    def received(src, c):
        parts = []
        for i in range(blocks):
            at = kvh * tall + 16 * i
            pair = src[c, at:at + 16].astype(F32)
            parts.append(pair[0:8] + pair[8:16])
        return parts[0] if blocks == 1 else jnp.concatenate(parts, axis=1)

    def emit(c, dst, extra):
        pack = jnp.zeros((tall, HD), F32)
        for h in range(kvh):
            pack = jnp.where(lanes == h, jnp.sum(den[h], axis=-1, keepdims=True), pack)
        dens = pack.T[0:8]
        if extra is not None:
            dens += received(extra, c)
        hi = dens.astype(BF16).astype(F32)
        both = jnp.concatenate([hi, dens - hi], axis=0).astype(BF16)
        for i in range(blocks):
            at = kvh * tall + 16 * i
            dst[c, at:at + 16] = both[:, i * HD:(i + 1) * HD]
        for h in range(kvh):
            x = num[h]
            if extra is not None:
                x += extra[c, h * tall:(h + 1) * tall].astype(F32)
            dst[c, h * tall:(h + 1) * tall] = x.astype(BF16)

    def relay(c):
        @pl.when(has_next)
        def _():
            q_near(c).wait_recv()

        @pl.when(has_next & has_prev)
        def _():
            q_far(c).start()

    def far(c):
        q_far(c).wait_recv()

        @pl.when(odd == 0)
        def _():
            unit(q4, c, [(0, 2), (1, 0)], num, den)

        @pl.when(odd == 1)
        def _():
            unit(q4, c, [(0, 2)], num, den)

        emit(c, fs, None)
        p_far(c).start()

    def near(c):
        unit(q2, c, [(0, 0), (1, 0)], num, den)

        @pl.when(has_prev)
        def _():
            p_far(c).wait_recv()

        emit(c, ns, fr)
        p_near(c).start()

    def own(c):
        @pl.when(odd == 0)
        def _():
            unit(q0, c, [(0, 1)], acc.at[c], accd.at[c])

        @pl.when(odd == 1)
        def _():
            unit(q0, c, [(0, 1), (1, 0)], acc.at[c], accd.at[c])

    def finish(f):
        for z in range(G):
            c = f * G + z

            @pl.when(has_prev)
            def _():
                p_near(c).wait_recv()

            dens = received(nr, c)
            dens = jnp.concatenate([dens, jnp.zeros((HD - 8, tall), F32)], axis=0).T
            for h in range(kvh):
                total = jnp.sum(accd[c, h], axis=-1, keepdims=True) + dens[:, h:h + 1]
                top = acc[c, h] + nr[c, h * tall:(h + 1) * tall].astype(F32)
                a = (top * (1.0 / total)).astype(BF16)
                for g in range(2):
                    at = (2 * h + g) * HD
                    att[z * chunk:(z + 1) * chunk, at:at + HD] = a[g * chunk:(g + 1) * chunk]

        def column(i, inner):
            cs = pl.ds(pl.multiple_of(i * NT, NT), NT)
            y = jnp.dot(att[...], wob[:, cs], preferred_element_type=F32).astype(BF16)
            for z in range(G):
                proj[f, :, :, z, :, cs] = y[z * chunk:(z + 1) * chunk].reshape(ny, nx, sub, NT)
            return inner

        lax.fori_loop(0, d // NT, column, 0)
        for cp in first_phase(f):
            cp.start()

    def middle(c):
        for cp in first_phase(c):
            cp.wait_recv()
        for y in range(ny):
            part = proj[c, y, x_own, :, :, 0:half].astype(F32)
            for k in range(1, nx):
                part += ra1[c, k - 1, y].astype(F32)
            pa[c, y] = part.astype(BF16)
        for x in range(nx):
            part = proj[c, y_own, x, :, :, half:d].astype(F32)
            for k in range(1, ny):
                part += rb1[c, k - 1, x].astype(F32)
            pb[c, x] = part.astype(BF16)
        for cp in second_phase(c):
            cp.start()

    def out_copy(c):
        return pltpu.make_async_copy(
            obuf.at[c], out.at[pl.ds(pl.multiple_of(c * G * sub, G * sub), G * sub)], osem.at[c])

    def close(c):
        for cp in second_phase(c):
            cp.wait_recv()
        lo = pa[c, y_own].astype(F32)
        for k in range(1, ny):
            lo += ra2[c, k - 1].astype(F32)
        hi = pb[c, x_own].astype(F32)
        for k in range(1, nx):
            hi += rb2[c, k - 1].astype(F32)
        lo = lo.reshape(G * sub, half)
        hi = hi.reshape(G * sub, half)
        squares = jnp.sum(lo * lo, axis=-1, keepdims=True) + jnp.sum(hi * hi, axis=-1, keepdims=True)
        scale = lax.rsqrt(squares / d + 0.1)
        span = pl.ds(pl.multiple_of(c * G * sub, G * sub), G * sub)
        for v, at in ((lo, slice(0, half)), (hi, slice(half, d))):
            r = res[span, at].astype(F32)
            obuf[c, :, at] = (r + v * scale * post_gain[:, at]).astype(BF16)
        out_copy(c).start()

    wo_copy.wait()
    res_copy.wait()

    def step(k, carry):
        @pl.when(k < NC)
        def _():
            relay(k)

        @pl.when(has_prev & (k + 2 < NC))
        def _():
            q_near(k + 2).start()

        @pl.when(has_far & (k >= 1) & (k <= NC))
        def _():
            far(k - 1)

        @pl.when(has_next & (k >= 2) & (k <= NC + 1))
        def _():
            near(k - 2)

        @pl.when(k < NC)
        def _():
            own(k)

        even = lax.rem(k, G) == 0

        @pl.when(even & (k >= G + 2))
        def _():
            finish((k - 2 - G) // G)

        @pl.when((lax.rem(k, G) == G - 1) & (k >= 2 * G + 1))
        def _():
            middle((k - 2 * G - 1) // G)

        @pl.when((lax.rem(k, G) == G - 1) & (k >= 3 * G + 1))
        def _():
            close((k - 3 * G - 1) // G)

        return carry

    lax.fori_loop(0, NC + 3, step, 0)
    close(NF - 2)
    middle(NF - 1)
    close(NF - 1)

    def drain(h, carry):
        for cp in kv_partner(h):
            cp.wait_send()
        return carry

    lax.fori_loop(0, kvh, drain, 0)

    def drain_chunks(c, carry):
        @pl.when(has_prev)
        def _():
            q_near(c).wait_send()

        @pl.when(has_next & has_prev)
        def _():
            q_far(c).wait_send()

        @pl.when(has_far)
        def _():
            p_far(c).wait_send()

        @pl.when(has_next)
        def _():
            p_near(c).wait_send()

        return carry

    lax.fori_loop(0, NC, drain_chunks, 0)

    def drain_out(c, carry):
        for cp in first_phase(c) + second_phase(c):
            cp.wait_send()
        out_copy(c).wait()
        return carry

    lax.fori_loop(0, NF, drain_out, 0)


def shards(n, n_tp, hidden_in, pre_gain, w_query, key_cache, value_cache, w_out, post_gain, starts, counts):
    rows, d = hidden_in.shape
    ctx, kvw = key_cache.shape
    kvh = kvw // HD
    sub = SUB
    NC = rows // (n_tp * sub)
    NF = NC // G
    chunk = rows // NC
    tall = 2 * chunk
    nx, ny, half = 2, n_tp // 2, d // 2
    dma = pltpu.SemaphoreType.DMA
    kv = pltpu.VMEM((2, kvh, ctx, HD), BF16)
    queries = pltpu.VMEM((NC, kvh, tall, HD), BF16)
    partial = pltpu.VMEM((NC, kvh * tall + 16 * (tall // HD), HD), BF16)
    any_spec = pl.BlockSpec(memory_space=pl.ANY)
    vmem_spec = pl.BlockSpec(memory_space=pltpu.VMEM)
    smem_spec = pl.BlockSpec(memory_space=pltpu.SMEM)
    return pl.pallas_call(
        functools.partial(kernel, n, n_tp, kvh, NC),
        out_shape=jax.ShapeDtypeStruct((rows // n_tp, d), BF16),
        in_specs=[smem_spec, smem_spec, any_spec, vmem_spec] + [any_spec] * 4 + [vmem_spec],
        out_specs=any_spec,
        scratch_shapes=[
            pltpu.VMEM((NC, n_tp, sub, d), BF16),
            pltpu.VMEM((kvh, d, 2 * HD), BF16),
            pltpu.VMEM(w_out.shape, BF16),
            kv,
            pltpu.VMEM((2, kvh, HD, ctx), BF16),
            kv,
            queries, queries, queries,
            partial, partial, partial, partial,
            pltpu.VMEM((NC, kvh, tall, HD), F32),
            pltpu.VMEM((NC, kvh, tall, HD), F32),
            pltpu.VMEM((kvh, tall, HD), F32),
            pltpu.VMEM((kvh, tall, HD), F32),
            pltpu.VMEM((tall, KB), jnp.int32),
            pltpu.VMEM((tall, KT), F32), pltpu.VMEM((tall, KT), F32),
            pltpu.VMEM((tall, KT), BF16), pltpu.VMEM((tall, KT), BF16),
            pltpu.VMEM((NF, ny, nx, G, sub, d), BF16),
            pltpu.VMEM((NF, nx - 1, ny, G, sub, half), BF16),
            pltpu.VMEM((NF, ny, G, sub, half), BF16),
            pltpu.VMEM((NF, ny - 1, G, sub, half), BF16),
            pltpu.VMEM((NF, ny - 1, nx, G, sub, half), BF16),
            pltpu.VMEM((NF, nx, G, sub, half), BF16),
            pltpu.VMEM((NF, nx - 1, G, sub, half), BF16),
            pltpu.VMEM((rows // n_tp, d), BF16),
            pltpu.VMEM((NF, G * sub, d), BF16),
            pltpu.VMEM((G * chunk, w_out.shape[0]), BF16),
            dma((NC, n_tp)), dma((kvh,)), dma, dma((kvh, 2)), dma, dma((NF,)),
            dma((kvh, 2)), dma((kvh, 2)),
            dma((NC,)), dma((NC,)), dma((NC,)), dma((NC,)),
            dma((NC,)), dma((NC,)), dma((NC,)), dma((NC,)),
            dma((NF, nx - 1)), dma((NF, nx - 1)), dma((NF, ny - 1)), dma((NF, ny - 1)),
            dma((NF, ny - 1)), dma((NF, ny - 1)), dma((NF, nx - 1)), dma((NF, nx - 1)),
        ],
        compiler_params=pltpu.CompilerParams(
            collective_id=0, has_side_effects=True, vmem_limit_bytes=67_000_000),
        name="attention_block",
    )(starts, counts, hidden_in, pre_gain.reshape(1, d), w_query, key_cache, value_cache, w_out,
      post_gain.reshape(1, d))


def solution(mesh):
    return jax.shard_map(
        functools.partial(shards, mesh.shape["seq"], mesh.shape["tp"]),
        mesh=mesh,
        in_specs=(
            P("seq", None),
            P(),
            P(None, "tp"),
            P("seq", "tp"),
            P("seq", "tp"),
            P("tp", None),
            P(),
            P(),
            P(),
        ),
        out_specs=P(("seq", "tp"), None),
        check_vma=False,
    )
```

time: 112 us -> 105 us (0.938)
  the two profiles are of different devices: /device:TPU:16 before, /device:TPU:0 now
where the time goes in v1:
time: 105 us; the launch traced here: 104 us
  Pallas kernels  99.4 us (95%)
  local copies, waits for them, and re-layouts  5.04 us (5%)
    pallas_call x1, Pallas kernels, shards(): pl.pallas_call(functools.partial(kernel, n, n_tp, kvh, NC), out_shape=jax...  99.4 us
    unnamed x1, local copies, waits for them, and re-layouts  2.36 us

profile of v1, /device:TPU:0, one launch (start us, length us, event | category | flops | bytes accessed | tf_op | source)
XLA Modules:
  0.0 104.4 jit_solution(11323703787622350007)
XLA Ops:
  0.0 1.3 %reshape.6.pre_gain = f32[1,4608]{1,0:T(1,128)} reshape(f32[4608]{0:T(1024)} %param.10) | data formatting | bytes 36864 | tf_op jit(solution)/shard_map/reshape | solution.py:569
  1.3 1.3 %reshape.7.post_gain = f32[1,4608]{1,0:T(1,128)} reshape(f32[4608]{0:T(1024)} %param.15) | data formatting | bytes 36864 | tf_op jit(solution)/shard_map/reshape | solution.py:570
  2.7 99.4 %attention_block.1 = bf16[128,4608]{1,0:T(8,128)(2,1)} custom-call(s32[8]{0:T(128)} %starts.1, s32[8]{0:T(128)} %counts.1, bf16[512,4608]{1,0:T(8,128)(2,1)} %hidden.1, f32[1,4608]{1,0:T(1,128)} %reshape.6.pre_gain, bf16[4608,1024]{1,0:T(8,128)(2,1)} %wq.1, bf16[1024,512]{1,0:T(8,128)(2,1)} %key.1, bf16[1024,512]{1,0:T(8,128)(2,1)} %value.1, ...), custom_call_target="tpu_custom_call" | custom-call | tf_op jit(solution)/shard_map/attention_block/pallas_call | solution.py:528
  102.0 2.4 %copy.11 = bf16[128,4608]{1,0:T(8,128)(2,1)} copy(bf16[128,4608]{1,0:T(8,128)(2,1)} %attention_block.1) | data formatting | bytes 2359296

commit v2 on v1

--- a/solution.py
+++ b/solution.py
@@ -25,10 +25,10 @@
 
 def kernel(
     n, n_tp, kvh, NC,
-    starts, counts, hidden, pre_gain, wq, key, value, wout, post_gain, out,
-    hbuf, wqb, wob, kraw, kt, vb, q0, q2, q4, fs, fr, ns, nr, acc, accd, num, den, rel, sc0, sc1, pw0, pw1,
+    starts, counts, hidden, gain_in, wq, key, value, wout, gain_out, out,
+    hbuf, wqb, wob, kraw, kt, vb, q0, q2, q4, fs, fr, ns, nr, acc, accd, num, den, numf, denf, rel, sc0, sc1, pw0, pw1, rms, pre_gain, post_gain,
     proj, ra1, pa, ra2, rb1, pb, rb2, res, obuf, att,
-    hsem, wqsem, wosem, kvsem, ressem, osem,
+    hsem, wqsem, wosem, kvsem, ressem, osem, gsem,
     s1, r1, sn, rn, sf, rf, sF, rF, sN, rN,
     sa1, ta1, sa2, ta2, sb1, tb1, sb2, tb2,
 ):
@@ -49,6 +49,19 @@
     has_next = s + 2 < n
     has_far = s + 4 < n
 
+    barrier = pltpu.get_barrier_semaphore()
+    pl.semaphore_signal(barrier, inc=1, device_id=(partner, t), device_id_type=MESH)
+    for k in range(1, n_tp):
+        pl.semaphore_signal(barrier, inc=1, device_id=(s, lax.rem(t + k, n_tp)), device_id_type=MESH)
+
+    @pl.when(has_prev)
+    def _():
+        pl.semaphore_signal(barrier, inc=1, device_id=(s - 2, t), device_id_type=MESH)
+
+    @pl.when(has_next)
+    def _():
+        pl.semaphore_signal(barrier, inc=1, device_id=(s + 2, t), device_id_type=MESH)
+
     def h_copy(c, b):
         return pltpu.make_async_copy(
             hidden.at[pl.ds(pl.multiple_of(b * owned + c * sub, sub), sub)], hbuf.at[c, b], hsem.at[c, b])
@@ -66,33 +79,17 @@
             for j, (src, dst) in enumerate(((key, kraw), (value, vb)))
         ]
 
-    for c in range(NC // 2):
+    gains = [
+        pltpu.make_async_copy(src, dst.at[0], gsem.at[i])
+        for i, (src, dst) in enumerate(((gain_in, pre_gain), (gain_out, post_gain)))
+    ]
+    for cp in gains:
+        cp.start()
+    for c in range(2):
         for b in range(n_tp):
             h_copy(c, b).start()
     for h in range(kvh):
         wq_copy(h).start()
-    for c in range(NC // 2, NC):
-        for b in range(n_tp):
-            h_copy(c, b).start()
-    for h in range(kvh):
-        for cp in kv_local(h):
-            cp.start()
-
-    barrier = pltpu.get_barrier_semaphore()
-    pl.semaphore_signal(barrier, inc=1, device_id=(partner, t), device_id_type=MESH)
-    for k in range(1, n_tp):
-        pl.semaphore_signal(barrier, inc=1, device_id=(s, lax.rem(t + k, n_tp)), device_id_type=MESH)
-
-    @pl.when(has_prev)
-    def _():
-        pl.semaphore_signal(barrier, inc=1, device_id=(s - 2, t), device_id_type=MESH)
-
-    @pl.when(has_next)
-    def _():
-        pl.semaphore_signal(barrier, inc=1, device_id=(s + 2, t), device_id_type=MESH)
-
-    pl.semaphore_wait(
-        barrier, n_tp + jnp.where(has_prev, 1, 0) + jnp.where(has_next, 1, 0))
 
     def kv_partner(h):
         return [
@@ -154,14 +151,9 @@
                 y_own * nx + xt))
         return copies
 
-    for h in range(kvh):
-        for cp in kv_partner(h):
-            cp.start()
     wo_copy = pltpu.make_async_copy(wout, wob, wosem)
-    wo_copy.start()
     res_copy = pltpu.make_async_copy(
         hidden.at[pl.ds(pl.multiple_of(t * owned, owned), owned)], res, ressem)
-    res_copy.start()
 
     shape = (2, n_tp, sub, KB)
     rel[...] = (
@@ -175,39 +167,65 @@
         fr[...] = jnp.zeros_like(fr)
         nr[...] = jnp.zeros_like(nr)
 
-    def queries(c0, count):
+    def queries(c0, first):
+        def arrive(i, carry):
+            h_copy(c0 + i // n_tp, i % n_tp).wait()
+            return carry
+
+        lax.fori_loop(0, 2 * n_tp, arrive, 0)
+
+        def scale(i, carry):
+            x = hbuf[c0 + i // n_tp, i % n_tp].astype(F32)
+            r = lax.rsqrt(jnp.mean(x * x, axis=-1, keepdims=True) + 0.1)
+            rms[i] = jnp.broadcast_to(r, (sub, HD))
+            return carry
+
+        lax.fori_loop(0, 2 * n_tp, scale, 0, unroll=4)
+        if first:
+            for cp in gains:
+                cp.wait()
+
         def norm(i, carry):
             c = c0 + i // n_tp
             b = i % n_tp
-            h_copy(c, b).wait()
-            x = hbuf[c, b].astype(F32)
-            y = x * lax.rsqrt(jnp.mean(x * x, axis=-1, keepdims=True) + 0.1) * pre_gain[...]
-            hbuf[c, b] = y.astype(BF16)
+            r = rms[i]
+            for k in range(0, d, HD):
+                x = hbuf[c, b, :, k:k + HD].astype(F32)
+                hbuf[c, b, :, k:k + HD] = (x * r * pre_gain[:, k:k + HD]).astype(BF16)
             return carry
 
-        lax.fori_loop(0, count * n_tp, norm, 0, unroll=4)
+        lax.fori_loop(0, 2 * n_tp, norm, 0)
+        if first:
+            pl.semaphore_wait(
+                barrier, n_tp + jnp.where(has_prev, 1, 0) + jnp.where(has_next, 1, 0))
+            for h in range(kvh):
+                for cp in kv_local(h):
+                    cp.start()
+            for h in range(kvh):
+                for cp in kv_partner(h):
+                    cp.start()
+            for c in range(2, NC):
+                for b in range(n_tp):
+                    h_copy(c, b).start()
 
         def project(h, carry):
-            if c0 == 0:
+            if first:
                 wq_copy(h).wait()
-            x = hbuf[c0:c0 + count].reshape(count * chunk, d)
+            x = hbuf[pl.ds(c0, 2)].reshape(2 * chunk, d)
             y = jnp.dot(x, wqb[h], preferred_element_type=F32) * ((d // HEADS) ** -0.5 / SOFT)
             y = y.astype(BF16)
-            for i in range(count):
+            for i in range(2):
                 q0[c0 + i, h, 0:chunk] = y[i * chunk:(i + 1) * chunk, :HD]
                 q0[c0 + i, h, chunk:tall] = y[i * chunk:(i + 1) * chunk, HD:]
             return carry
 
-        lax.fori_loop(0, kvh, project, 0)
-
-    queries(0, NC // 2)
-
+        lax.fori_loop(0, kvh, project, 0, unroll=1 if first else 2)
+
+    queries(0, True)
     @pl.when(has_prev)
     def _():
         q_near(0).start()
         q_near(1).start()
-
-    queries(NC // 2, NC // 2)
 
     def turn(src):
         def body(h, carry):
@@ -221,7 +239,10 @@
 
         lax.fori_loop(0, kvh, body, 0)
 
+    wo_copy.start()
+    res_copy.start()
     turn(0)
+    queries(2, False)
     turn(1)
 
     off_own = starts[s] - s * ctx
@@ -231,61 +252,56 @@
     fill1 = counts[partner]
     lane = lax.broadcasted_iota(jnp.int32, (1, KB), 1)
 
-    def unit(q, c, sources, num, den):
-        tiles = [
-            (h, src, mode, i)
-            for h in range(kvh) for src, mode in sources for i in range(ctx // KT)
-        ]
-        last = len(sources) * (ctx // KT)
-        tops = {}
-        belows = {}
-
-        def scores(j):
-            h, src, mode, i = tiles[j]
-            qt = q[c, h]
-            for b in range(0, KT, KB):
-                at = i * KT + b
-                sc[j % 2][:, b:b + KB] = jnp.dot(
-                    qt, kt[src, h, :, at:at + KB], preferred_element_type=F32)
-
-        def weights(j):
-            h, src, mode, i = tiles[j]
+    def unit(*parts):
+        tiles = []
+        for q, c, sources, num, den in parts:
+            for h in range(kvh):
+                spans = [(src, mode, i) for src, mode in sources for i in range(0, ctx, KT)]
+                sums = [None, None]
+                for j, (src, mode, i) in enumerate(spans):
+                    tiles.append((q, c, num, den, h, src, mode, i, sums, j == len(spans) - 1))
+
+        def scores(j, b):
+            q, c, num, den, h, src, mode, i, sums, last = tiles[j]
+            sc[j % 2][:, b:b + KB] = jnp.dot(
+                q[c, h], kt[src, h, :, i + b:i + b + KB], preferred_element_type=F32)
+
+        def weights(j, b):
+            q, c, num, den, h, src, mode, i, sums, last = tiles[j]
             fill = fill1 if src else fill0
-            below = belows.get(h)
-            for b in range(0, KT, KB):
-                at = i * KT + b
-                p = jnp.exp2(jnp.tanh(sc[j % 2][:, b:b + KB]) * GAIN)
-                if mode == 1:
-                    p = jnp.where(rel[...] <= off_own + c * sub - at, p, 0.0)
-                elif mode == 2:
-                    ok = (rel[...] > off_far + c * sub - at) & (lane < fill - at)
-                    p = jnp.where(ok, p, 0.0)
-                else:
-                    p = jnp.where(lane < fill - at, p, 0.0)
-                for k in range(0, KB, HD):
-                    part = p[:, k:k + HD]
-                    below = part if below is None else below + part
-                pw[j % 2][:, b:b + KB] = p.astype(BF16)
-            belows[h] = below
-            if j % last == last - 1:
-                den[h] = below
-
-        def values(j):
-            h, src, mode, i = tiles[j]
+            at = i + b
+            p = jnp.exp2(jnp.tanh(sc[j % 2][:, b:b + KB]) * GAIN)
+            if mode == 1:
+                p = jnp.where(rel[...] <= off_own + c * sub - at, p, 0.0)
+            elif mode == 2:
+                ok = (rel[...] > off_far + c * sub - at) & (lane < fill - at)
+                p = jnp.where(ok, p, 0.0)
+            else:
+                p = jnp.where(lane < fill - at, p, 0.0)
+            for k in range(0, KB, HD):
+                part = p[:, k:k + HD]
+                sums[0] = part if sums[0] is None else sums[0] + part
+            pw[j % 2][:, b:b + KB] = p.astype(BF16)
+            if last and b == KT - KB:
+                den[h] = sums[0]
+
+        def values(j, b):
+            q, c, num, den, h, src, mode, i, sums, last = tiles[j]
             a = jnp.dot(
-                pw[j % 2][...], vb[src, h, i * KT:(i + 1) * KT], preferred_element_type=F32)
-            tops[h] = tops[h] + a if h in tops else a
-            if j % last == last - 1:
-                num[h] = tops[h]
+                pw[j % 2][:, b:b + KB], vb[src, h, i + b:i + b + KB], preferred_element_type=F32)
+            sums[1] = a if sums[1] is None else sums[1] + a
+            if last and b == KT - KB:
+                num[h] = sums[1]
 
         count = len(tiles)
         for k in range(count + 2):
-            if k < count:
-                scores(k)
-            if 0 <= k - 1 < count:
-                weights(k - 1)
-            if 0 <= k - 2:
-                values(k - 2)
+            for b in range(0, KT, KB):
+                if k < count:
+                    scores(k, b)
+                if 0 <= k - 1 < count:
+                    weights(k - 1, b)
+                if 0 <= k - 2:
+                    values(k - 2, b)
 
     blocks = tall // HD
     lanes = lax.broadcasted_iota(jnp.int32, (tall, HD), 1)
@@ -298,7 +314,7 @@
             parts.append(pair[0:8] + pair[8:16])
         return parts[0] if blocks == 1 else jnp.concatenate(parts, axis=1)
 
-    def emit(c, dst, extra):
+    def emit(c, num, den, dst, extra):
         pack = jnp.zeros((tall, HD), F32)
         for h in range(kvh):
             pack = jnp.where(lanes == h, jnp.sum(den[h], axis=-1, keepdims=True), pack)
@@ -325,38 +341,35 @@
         def _():
             q_far(c).start()
 
-    def far(c):
-        q_far(c).wait_recv()
-
+    def far_part(c, even):
+        return q4, c, [(0, 2), (1, 0)] if even else [(0, 2)], numf, denf
+
+    def near_part(c):
+        return q2, c, [(0, 0), (1, 0)], num, den
+
+    def own_part(c, even):
+        return q0, c, [(0, 1)] if even else [(0, 1), (1, 0)], acc.at[c], accd.at[c]
+
+    def by_parity(body):
         @pl.when(odd == 0)
         def _():
-            unit(q4, c, [(0, 2), (1, 0)], num, den)
+            body(True)
 
         @pl.when(odd == 1)
         def _():
-            unit(q4, c, [(0, 2)], num, den)
-
-        emit(c, fs, None)
+            body(False)
+
+    def send_far(c):
+        emit(c, numf, denf, fs, None)
         p_far(c).start()
 
-    def near(c):
-        unit(q2, c, [(0, 0), (1, 0)], num, den)
-
+    def send_near(c):
         @pl.when(has_prev)
         def _():
             p_far(c).wait_recv()
 
-        emit(c, ns, fr)
+        emit(c, num, den, ns, fr)
         p_near(c).start()
-
-    def own(c):
-        @pl.when(odd == 0)
-        def _():
-            unit(q0, c, [(0, 1)], acc.at[c], accd.at[c])
-
-        @pl.when(odd == 1)
-        def _():
-            unit(q0, c, [(0, 1), (1, 0)], acc.at[c], accd.at[c])
 
     def finish(f):
         for z in range(G):
@@ -430,46 +443,69 @@
     res_copy.wait()
 
     def step(k, carry):
-        @pl.when(k < NC)
-        def _():
-            relay(k)
-
-        @pl.when(has_prev & (k + 2 < NC))
+        full = has_far & (k >= jnp.where(has_prev, 2, 1)) & (k < NC)
+
+        kn = k - jnp.where(has_prev, 2, 1)
+
+        @pl.when(has_prev & (k >= 0) & (k + 2 < NC))
         def _():
             q_near(k + 2).start()
 
+        @pl.when((k >= 0) & (k < NC) & jnp.logical_not(full))
+        def _():
+            by_parity(lambda even: unit(own_part(k, even)))
+
         @pl.when(has_far & (k >= 1) & (k <= NC))
         def _():
-            far(k - 1)
-
-        @pl.when(has_next & (k >= 2) & (k <= NC + 1))
-        def _():
-            near(k - 2)
-
-        @pl.when(k < NC)
-        def _():
-            own(k)
-
-        even = lax.rem(k, G) == 0
-
-        @pl.when(even & (k >= G + 2))
-        def _():
-            finish((k - 2 - G) // G)
-
-        @pl.when((lax.rem(k, G) == G - 1) & (k >= 2 * G + 1))
-        def _():
-            middle((k - 2 * G - 1) // G)
-
-        @pl.when((lax.rem(k, G) == G - 1) & (k >= 3 * G + 1))
-        def _():
-            close((k - 3 * G - 1) // G)
+            q_far(k - 1).wait_recv()
+
+        @pl.when(full)
+        def _():
+            by_parity(lambda even: unit(far_part(k - 1, even), near_part(kn), own_part(k, even)))
+
+        @pl.when(has_far & (k >= 1) & (k <= NC) & jnp.logical_not(full))
+        def _():
+            by_parity(lambda even: unit(far_part(k - 1, even)))
+
+        @pl.when(has_far & (k >= 1) & (k <= NC))
+        def _():
+            send_far(k - 1)
+
+        @pl.when(k + 1 < NC)
+        def _():
+            relay(k + 1)
+
+        @pl.when(has_next & (kn >= 0) & (kn < NC) & jnp.logical_not(full))
+        def _():
+            unit(near_part(kn))
+
+        @pl.when(has_next & (kn >= 0) & (kn < NC))
+        def _():
+            send_near(kn)
+
+        @pl.when((k >= 1) & (lax.rem(k, 2) == 1) & (k + 3 < NC))
+        def _():
+            queries(k + 3, False)
+
+        @pl.when((k >= G + 2) & (lax.rem(k - 2, G) == 0))
+        def _():
+            finish((k - G - 2) // G)
+
+        @pl.when((k >= G + 4) & (lax.rem(k - 4, G) == 0))
+        def _():
+            middle((k - G - 4) // G)
+
+        @pl.when((k >= 2 * G + 4) & (lax.rem(k - 4, G) == 0))
+        def _():
+            close((k - 2 * G - 4) // G)
 
         return carry
 
-    lax.fori_loop(0, NC + 3, step, 0)
-    close(NF - 2)
-    middle(NF - 1)
-    close(NF - 1)
+    lax.fori_loop(-1, NC + 3, step, 0)
+    rest = [(G * f + 2 * G + 4, 0, f) for f in range(NF)] + [(G * f + G + 4, 1, f) for f in range(NF)]
+    for at, kind, f in sorted(rest):
+        if at >= NC + 3:
+            (close, middle)[kind](f)
 
     def drain(h, carry):
         for cp in kv_partner(h):
@@ -523,12 +559,11 @@
     queries = pltpu.VMEM((NC, kvh, tall, HD), BF16)
     partial = pltpu.VMEM((NC, kvh * tall + 16 * (tall // HD), HD), BF16)
     any_spec = pl.BlockSpec(memory_space=pl.ANY)
-    vmem_spec = pl.BlockSpec(memory_space=pltpu.VMEM)
     smem_spec = pl.BlockSpec(memory_space=pltpu.SMEM)
     return pl.pallas_call(
         functools.partial(kernel, n, n_tp, kvh, NC),
         out_shape=jax.ShapeDtypeStruct((rows // n_tp, d), BF16),
-        in_specs=[smem_spec, smem_spec, any_spec, vmem_spec] + [any_spec] * 4 + [vmem_spec],
+        in_specs=[smem_spec, smem_spec] + [any_spec] * 7,
         out_specs=any_spec,
         scratch_shapes=[
             pltpu.VMEM((NC, n_tp, sub, d), BF16),
@@ -543,9 +578,13 @@
             pltpu.VMEM((NC, kvh, tall, HD), F32),
             pltpu.VMEM((kvh, tall, HD), F32),
             pltpu.VMEM((kvh, tall, HD), F32),
+            pltpu.VMEM((kvh, tall, HD), F32),
+            pltpu.VMEM((kvh, tall, HD), F32),
             pltpu.VMEM((tall, KB), jnp.int32),
             pltpu.VMEM((tall, KT), F32), pltpu.VMEM((tall, KT), F32),
             pltpu.VMEM((tall, KT), BF16), pltpu.VMEM((tall, KT), BF16),
+            pltpu.VMEM((2 * n_tp, sub, HD), F32),
+            pltpu.VMEM((1, d), F32), pltpu.VMEM((1, d), F32),
             pltpu.VMEM((NF, ny, nx, G, sub, d), BF16),
             pltpu.VMEM((NF, nx - 1, ny, G, sub, half), BF16),
             pltpu.VMEM((NF, ny, G, sub, half), BF16),
@@ -556,7 +595,7 @@
             pltpu.VMEM((rows // n_tp, d), BF16),
             pltpu.VMEM((NF, G * sub, d), BF16),
             pltpu.VMEM((G * chunk, w_out.shape[0]), BF16),
-            dma((NC, n_tp)), dma((kvh,)), dma, dma((kvh, 2)), dma, dma((NF,)),
+            dma((NC, n_tp)), dma((kvh,)), dma, dma((kvh, 2)), dma, dma((NF,)), dma((2,)),
             dma((kvh, 2)), dma((kvh, 2)),
             dma((NC,)), dma((NC,)), dma((NC,)), dma((NC,)),
             dma((NC,)), dma((NC,)), dma((NC,)), dma((NC,)),
@@ -566,8 +605,7 @@
         compiler_params=pltpu.CompilerParams(
             collective_id=0, has_side_effects=True, vmem_limit_bytes=67_000_000),
         name="attention_block",
-    )(starts, counts, hidden_in, pre_gain.reshape(1, d), w_query, key_cache, value_cache, w_out,
-      post_gain.reshape(1, d))
+    )(starts, counts, hidden_in, pre_gain, w_query, key_cache, value_cache, w_out, post_gain)
 
 
 def solution(mesh):

time: 105 us -> 94.8 us (0.903)
  Pallas kernels: 99.4 us -> 92.3 us
  local copies, waits for them, and re-layouts: 5.04 us -> 2.36 us
    pallas_call x1, Pallas kernels: 99.4 us -> 92.3 us  [shards(): pl.pallas_call(functools.partial(kernel, n, n_tp, kvh, NC), out_shape=jax...]
    reshape x2 -> x0, local copies, waits for them, and re-layouts: 2.68 us -> none  [the longest x1 1.35 us: shards(): pre_gain.reshape(1, d)]
where the time goes in v2:
time: 94.8 us; the launch traced here: 94.6 us
  Pallas kernels  92.3 us (97%)
  local copies, waits for them, and re-layouts  2.36 us (2%)
    pallas_call x1, Pallas kernels, shards(): pl.pallas_call(functools.partial(kernel, n, n_tp, kvh, NC), out_shape=jax...  92.3 us
    unnamed x1, local copies, waits for them, and re-layouts  2.36 us

profile of v2, /device:TPU:0, one launch (start us, length us, event | category | flops | bytes accessed | tf_op | source)
XLA Modules:
  0.0 94.6 jit_solution(17169062841132608941)
XLA Ops:
  0.0 92.3 %attention_block.1 = bf16[128,4608]{1,0:T(8,128)(2,1)} custom-call(s32[8]{0:T(128)} %starts.1, s32[8]{0:T(128)} %counts.1, bf16[512,4608]{1,0:T(8,128)(2,1)} %hidden.1, f32[4608]{0:T(1024)} %gain_in.1, bf16[4608,1024]{1,0:T(8,128)(2,1)} %wq.1, bf16[1024,512]{1,0:T(8,128)(2,1)} %key.1, bf16[1024,512]{1,0:T(8,128)(2,1)} %value.1, bf16[1024,4608]{1,0:T(8,128)(2,1)} %wout.1, ...), custom_call_target="tpu_custom_call" | custom-call | tf_op jit(solution)/shard_map/attention_block/pallas_call | solution.py:563
  92.3 2.4 %copy.11 = bf16[128,4608]{1,0:T(8,128)(2,1)} copy(bf16[128,4608]{1,0:T(8,128)(2,1)} %attention_block.1) | data formatting | bytes 2359296

commit v3 on v2

--- a/solution.py
+++ b/solution.py
@@ -12,8 +12,8 @@
 HD = 128
 WINDOW = 4096
 SUB = 16
-G = 2
 KB = 256
+UP = 1
 KT = 512
 NT = 2304
 SOFT = 50.0
@@ -26,10 +26,10 @@
 def kernel(
     n, n_tp, kvh, NC,
     starts, counts, hidden, gain_in, wq, key, value, wout, gain_out, out,
-    hbuf, wqb, wob, kraw, kt, vb, q0, q2, q4, fs, fr, ns, nr, acc, accd, num, den, numf, denf, rel, sc0, sc1, pw0, pw1, rms, pre_gain, post_gain,
+    hbuf, wqb, wob, kraw, kt, vb, kx, ktx, vx, q0, q2, q4, fs, fr, ns, nr, acc, accd, num, den, numf, denf, rel, sc0, sc1, pw0, pw1, rms, pre_gain, post_gain,
     proj, ra1, pa, ra2, rb1, pb, rb2, res, obuf, att,
     hsem, wqsem, wosem, kvsem, ressem, osem, gsem,
-    s1, r1, sn, rn, sf, rf, sF, rF, sN, rN,
+    s1, r1, su, ru, sr, rr, sn, rn, sf, rf, sF, rF, sN, rN,
     sa1, ta1, sa2, ta2, sb1, tb1, sb2, tb2,
 ):
     sc = (sc0, sc1)
@@ -44,7 +44,6 @@
     chunk = rows // NC
     tall = 2 * chunk
     owned = rows // n_tp
-    NF = NC // G
     has_prev = s >= 2
     has_next = s + 2 < n
     has_far = s + 4 < n
@@ -99,16 +98,34 @@
             for j, (src, dst) in enumerate(((key, kraw), (value, vb)))
         ]
 
-    def along(src, dst, send, recv, to):
+    def along(src, dst, send, recv, to, first=0):
+        span = pl.ds(first, src.shape[1] - first)
+
         def make(c):
             return pltpu.make_async_remote_copy(
-                src.at[c], dst.at[c], send.at[c], recv.at[c],
+                src.at[c, span], dst.at[c, span], send.at[c], recv.at[c],
                 device_id=(to, t), device_id_type=MESH)
         return make
 
+    def kv_up(h):
+        return [
+            pltpu.make_async_remote_copy(
+                src.at[:, cols(h)], dst.at[0, h], su.at[h, j], ru.at[h, j],
+                device_id=(s + 2, t), device_id_type=MESH)
+            for j, (src, dst) in enumerate(((key, kx), (value, vx)))
+        ]
+
+    def kv_across(h):
+        return [
+            pltpu.make_async_remote_copy(
+                ref.at[0, h], ref.at[1, h], sr.at[h, j], rr.at[h, j],
+                device_id=(partner, t), device_id_type=MESH)
+            for j, ref in enumerate((kx, vx))
+        ]
+
     q_near = along(q0, q2, sn, rn, s - 2)
-    q_far = along(q2, q4, sf, rf, s - 2)
-    p_far = along(fs, fr, sF, rF, s + 2)
+    q_far = along(q2, q4, sf, rf, s - 2, UP)
+    p_far = along(fs, fr, sF, rF, s + 2, UP * tall)
     p_near = along(ns, nr, sN, rN, s + 2)
 
     nx = 2
@@ -123,31 +140,33 @@
         return pltpu.make_async_remote_copy(
             src, dst, send, recv, device_id=(s, to), device_id_type=MESH)
 
-    def first_phase(c):
+    def first_phase(c, count):
+        span = pl.ds(c, count)
         copies = []
         for k in range(1, nx):
             xt = lax.rem(x_own + k, nx)
             copies.append(remote(
-                proj.at[c, :, xt, :, :, left], ra1.at[c, k - 1], sa1.at[c, k - 1], ta1.at[c, k - 1],
+                proj.at[span, :, xt, :, left], ra1.at[k - 1, span], sa1.at[c, k - 1], ta1.at[c, k - 1],
                 y_own * nx + xt))
         for k in range(1, ny):
             yt = lax.rem(y_own + k, ny)
             copies.append(remote(
-                proj.at[c, yt, :, :, :, right], rb1.at[c, k - 1], sb1.at[c, k - 1], tb1.at[c, k - 1],
+                proj.at[span, yt, :, :, right], rb1.at[k - 1, span], sb1.at[c, k - 1], tb1.at[c, k - 1],
                 yt * nx + x_own))
         return copies
 
-    def second_phase(c):
+    def second_phase(c, count):
+        span = pl.ds(c, count)
         copies = []
         for k in range(1, ny):
             yt = lax.rem(y_own + k, ny)
             copies.append(remote(
-                pa.at[c, yt], ra2.at[c, k - 1], sa2.at[c, k - 1], ta2.at[c, k - 1],
+                pa.at[span, yt], ra2.at[k - 1, span], sa2.at[c, k - 1], ta2.at[c, k - 1],
                 yt * nx + x_own))
         for k in range(1, nx):
             xt = lax.rem(x_own + k, nx)
             copies.append(remote(
-                pb.at[c, xt], rb2.at[c, k - 1], sb2.at[c, k - 1], tb2.at[c, k - 1],
+                pb.at[span, xt], rb2.at[k - 1, span], sb2.at[c, k - 1], tb2.at[c, k - 1],
                 y_own * nx + xt))
         return copies
 
@@ -165,6 +184,8 @@
     @pl.when(s < 2)
     def _():
         fr[...] = jnp.zeros_like(fr)
+        ktx[...] = jnp.zeros_like(ktx)
+        vx[...] = jnp.zeros_like(vx)
         nr[...] = jnp.zeros_like(nr)
 
     def queries(c0, first):
@@ -198,6 +219,12 @@
         if first:
             pl.semaphore_wait(
                 barrier, n_tp + jnp.where(has_prev, 1, 0) + jnp.where(has_next, 1, 0))
+            @pl.when(has_next)
+            def _():
+                for h in range(UP):
+                    for cp in kv_up(h):
+                        cp.start()
+
             for h in range(kvh):
                 for cp in kv_local(h):
                     cp.start()
@@ -248,33 +275,40 @@
     off_own = starts[s] - s * ctx
     s_far = jnp.minimum(s + 4, n - 1)
     off_far = starts[s_far] - s_far * ctx + 4 * ctx - WINDOW
-    fill0 = counts[s]
-    fill1 = counts[partner]
+    s_next = jnp.minimum(s + 2, n - 1)
+    off_next = starts[s_next] - s_next * ctx + 4 * ctx - WINDOW
+    fills = (
+        counts[s],
+        counts[partner],
+        jnp.where(has_prev, counts[jnp.maximum(s - 2, 0)], 0),
+        jnp.where(has_prev, counts[jnp.maximum(s - 1, 0)], 0),
+    )
     lane = lax.broadcasted_iota(jnp.int32, (1, KB), 1)
 
     def unit(*parts):
         tiles = []
         for q, c, sources, num, den in parts:
             for h in range(kvh):
-                spans = [(src, mode, i) for src, mode in sources for i in range(0, ctx, KT)]
+                spans = [(src, mode, i) for src, mode in sources(h) for i in range(0, ctx, KT)]
                 sums = [None, None]
                 for j, (src, mode, i) in enumerate(spans):
                     tiles.append((q, c, num, den, h, src, mode, i, sums, j == len(spans) - 1))
 
         def scores(j, b):
             q, c, num, den, h, src, mode, i, sums, last = tiles[j]
-            sc[j % 2][:, b:b + KB] = jnp.dot(
-                q[c, h], kt[src, h, :, i + b:i + b + KB], preferred_element_type=F32)
+            k = kt[src, h, :, i + b:i + b + KB] if src < 2 else ktx[src - 2, h, :, i + b:i + b + KB]
+            sc[j % 2][:, b:b + KB] = jnp.dot(q[c, h], k, preferred_element_type=F32)
 
         def weights(j, b):
             q, c, num, den, h, src, mode, i, sums, last = tiles[j]
-            fill = fill1 if src else fill0
+            fill = fills[src]
             at = i + b
             p = jnp.exp2(jnp.tanh(sc[j % 2][:, b:b + KB]) * GAIN)
             if mode == 1:
                 p = jnp.where(rel[...] <= off_own + c * sub - at, p, 0.0)
-            elif mode == 2:
-                ok = (rel[...] > off_far + c * sub - at) & (lane < fill - at)
+            elif mode >= 2:
+                off = off_far if mode == 2 else off_next
+                ok = (rel[...] > off + c * sub - at) & (lane < fill - at)
                 p = jnp.where(ok, p, 0.0)
             else:
                 p = jnp.where(lane < fill - at, p, 0.0)
@@ -287,8 +321,8 @@
 
         def values(j, b):
             q, c, num, den, h, src, mode, i, sums, last = tiles[j]
-            a = jnp.dot(
-                pw[j % 2][:, b:b + KB], vb[src, h, i + b:i + b + KB], preferred_element_type=F32)
+            v = vb[src, h, i + b:i + b + KB] if src < 2 else vx[src - 2, h, i + b:i + b + KB]
+            a = jnp.dot(pw[j % 2][:, b:b + KB], v, preferred_element_type=F32)
             sums[1] = a if sums[1] is None else sums[1] + a
             if last and b == KT - KB:
                 num[h] = sums[1]
@@ -314,9 +348,9 @@
             parts.append(pair[0:8] + pair[8:16])
         return parts[0] if blocks == 1 else jnp.concatenate(parts, axis=1)
 
-    def emit(c, num, den, dst, extra):
+    def emit(c, num, den, dst, extra, least):
         pack = jnp.zeros((tall, HD), F32)
-        for h in range(kvh):
+        for h in range(least, kvh):
             pack = jnp.where(lanes == h, jnp.sum(den[h], axis=-1, keepdims=True), pack)
         dens = pack.T[0:8]
         if extra is not None:
@@ -326,9 +360,9 @@
         for i in range(blocks):
             at = kvh * tall + 16 * i
             dst[c, at:at + 16] = both[:, i * HD:(i + 1) * HD]
-        for h in range(kvh):
+        for h in range(least, kvh):
             x = num[h]
-            if extra is not None:
+            if extra is not None and h >= UP:
                 x += extra[c, h * tall:(h + 1) * tall].astype(F32)
             dst[c, h * tall:(h + 1) * tall] = x.astype(BF16)
 
@@ -342,13 +376,23 @@
             q_far(c).start()
 
     def far_part(c, even):
-        return q4, c, [(0, 2), (1, 0)] if even else [(0, 2)], numf, denf
-
-    def near_part(c):
-        return q2, c, [(0, 0), (1, 0)], num, den
+        def sources(h):
+            if h < UP:
+                return []
+            return [(0, 2), (1, 0)] if even else [(0, 2)]
+        return q4, c, sources, numf, denf
+
+    def near_part(c, even):
+        def sources(h):
+            return [(2, 3), (3 if even else 1, 0)] if h < UP else [(0, 0), (1, 0)]
+        return q2, c, sources, num, den
 
     def own_part(c, even):
-        return q0, c, [(0, 1)] if even else [(0, 1), (1, 0)], acc.at[c], accd.at[c]
+        def sources(h):
+            if h < UP:
+                return [(0, 1), (3 if even else 1, 0), (2, 0)]
+            return [(0, 1)] if even else [(0, 1), (1, 0)]
+        return q0, c, sources, acc.at[c], accd.at[c]
 
     def by_parity(body):
         @pl.when(odd == 0)
@@ -360,7 +404,7 @@
             body(False)
 
     def send_far(c):
-        emit(c, numf, denf, fs, None)
+        emit(c, numf, denf, fs, None, UP)
         p_far(c).start()
 
     def send_near(c):
@@ -368,12 +412,12 @@
         def _():
             p_far(c).wait_recv()
 
-        emit(c, num, den, ns, fr)
+        emit(c, num, den, ns, fr, 0)
         p_near(c).start()
 
-    def finish(f):
-        for z in range(G):
-            c = f * G + z
+    def finish(c0, count):
+        for z in range(count):
+            c = c0 + z
 
             @pl.when(has_prev)
             def _():
@@ -391,83 +435,105 @@
 
         def column(i, inner):
             cs = pl.ds(pl.multiple_of(i * NT, NT), NT)
-            y = jnp.dot(att[...], wob[:, cs], preferred_element_type=F32).astype(BF16)
-            for z in range(G):
-                proj[f, :, :, z, :, cs] = y[z * chunk:(z + 1) * chunk].reshape(ny, nx, sub, NT)
+            y = jnp.dot(
+                att[0:count * chunk], wob[:, cs], preferred_element_type=F32).astype(BF16)
+            for z in range(count):
+                proj[c0 + z, :, :, :, cs] = y[z * chunk:(z + 1) * chunk].reshape(ny, nx, sub, NT)
             return inner
 
         lax.fori_loop(0, d // NT, column, 0)
-        for cp in first_phase(f):
+        for cp in first_phase(c0, count):
             cp.start()
 
-    def middle(c):
-        for cp in first_phase(c):
+    def middle(c0, count):
+        for cp in first_phase(c0, count):
             cp.wait_recv()
-        for y in range(ny):
-            part = proj[c, y, x_own, :, :, 0:half].astype(F32)
-            for k in range(1, nx):
-                part += ra1[c, k - 1, y].astype(F32)
-            pa[c, y] = part.astype(BF16)
-        for x in range(nx):
-            part = proj[c, y_own, x, :, :, half:d].astype(F32)
-            for k in range(1, ny):
-                part += rb1[c, k - 1, x].astype(F32)
-            pb[c, x] = part.astype(BF16)
-        for cp in second_phase(c):
+        for z in range(count):
+            c = c0 + z
+            for y in range(ny):
+                part = proj[c, y, x_own, :, 0:half].astype(F32)
+                for k in range(1, nx):
+                    part += ra1[k - 1, c, y].astype(F32)
+                pa[c, y] = part.astype(BF16)
+            for x in range(nx):
+                part = proj[c, y_own, x, :, half:d].astype(F32)
+                for k in range(1, ny):
+                    part += rb1[k - 1, c, x].astype(F32)
+                pb[c, x] = part.astype(BF16)
+        for cp in second_phase(c0, count):
             cp.start()
 
     def out_copy(c):
         return pltpu.make_async_copy(
-            obuf.at[c], out.at[pl.ds(pl.multiple_of(c * G * sub, G * sub), G * sub)], osem.at[c])
-
-    def close(c):
-        for cp in second_phase(c):
+            obuf.at[c], out.at[pl.ds(pl.multiple_of(c * sub, sub), sub)], osem.at[c])
+
+    def close(c0, count):
+        for cp in second_phase(c0, count):
             cp.wait_recv()
-        lo = pa[c, y_own].astype(F32)
-        for k in range(1, ny):
-            lo += ra2[c, k - 1].astype(F32)
-        hi = pb[c, x_own].astype(F32)
-        for k in range(1, nx):
-            hi += rb2[c, k - 1].astype(F32)
-        lo = lo.reshape(G * sub, half)
-        hi = hi.reshape(G * sub, half)
-        squares = jnp.sum(lo * lo, axis=-1, keepdims=True) + jnp.sum(hi * hi, axis=-1, keepdims=True)
-        scale = lax.rsqrt(squares / d + 0.1)
-        span = pl.ds(pl.multiple_of(c * G * sub, G * sub), G * sub)
-        for v, at in ((lo, slice(0, half)), (hi, slice(half, d))):
-            r = res[span, at].astype(F32)
-            obuf[c, :, at] = (r + v * scale * post_gain[:, at]).astype(BF16)
-        out_copy(c).start()
+        for z in range(count):
+            c = c0 + z
+            lo = pa[c, y_own].astype(F32)
+            for k in range(1, ny):
+                lo += ra2[k - 1, c].astype(F32)
+            hi = pb[c, x_own].astype(F32)
+            for k in range(1, nx):
+                hi += rb2[k - 1, c].astype(F32)
+            squares = jnp.sum(lo * lo, axis=-1, keepdims=True) + jnp.sum(hi * hi, axis=-1, keepdims=True)
+            scale = lax.rsqrt(squares / d + 0.1)
+            span = pl.ds(pl.multiple_of(c * sub, sub), sub)
+            for v, at in ((lo, slice(0, half)), (hi, slice(half, d))):
+                r = res[span, at].astype(F32)
+                obuf[c, :, at] = (r + v * scale * post_gain[:, at]).astype(BF16)
+            out_copy(c).start()
 
     wo_copy.wait()
     res_copy.wait()
 
+    def lift():
+        for h in range(UP):
+            for cp in kv_up(h):
+                cp.wait_recv()
+
+        @pl.when(odd == 1)
+        def _():
+            for h in range(UP):
+                for cp in kv_across(h):
+                    cp.start()
+
+        for h in range(UP):
+            ktx[0, h] = kx[0, h].T
+
+        @pl.when(odd == 0)
+        def _():
+            for h in range(UP):
+                for cp in kv_across(h):
+                    cp.wait_recv()
+                ktx[1, h] = kx[1, h].T
+
     def step(k, carry):
-        full = has_far & (k >= jnp.where(has_prev, 2, 1)) & (k < NC)
-
         kn = k - jnp.where(has_prev, 2, 1)
+        nearby = has_next & (kn >= 0) & (kn < NC)
+        middling = (k >= 1) & (k <= NC)
+        full = has_far & nearby & middling
 
         @pl.when(has_prev & (k >= 0) & (k + 2 < NC))
         def _():
             q_near(k + 2).start()
 
-        @pl.when((k >= 0) & (k < NC) & jnp.logical_not(full))
-        def _():
-            by_parity(lambda even: unit(own_part(k, even)))
-
-        @pl.when(has_far & (k >= 1) & (k <= NC))
+        @pl.when(has_far & middling)
         def _():
             q_far(k - 1).wait_recv()
 
         @pl.when(full)
         def _():
-            by_parity(lambda even: unit(far_part(k - 1, even), near_part(kn), own_part(k, even)))
-
-        @pl.when(has_far & (k >= 1) & (k <= NC) & jnp.logical_not(full))
+            by_parity(lambda even: unit(
+                far_part(k - 1, even), near_part(kn, even), own_part(k - 1, even)))
+
+        @pl.when(has_far & middling & jnp.logical_not(full))
         def _():
             by_parity(lambda even: unit(far_part(k - 1, even)))
 
-        @pl.when(has_far & (k >= 1) & (k <= NC))
+        @pl.when(has_far & middling)
         def _():
             send_far(k - 1)
 
@@ -475,37 +541,77 @@
         def _():
             relay(k + 1)
 
-        @pl.when(has_next & (kn >= 0) & (kn < NC) & jnp.logical_not(full))
-        def _():
-            unit(near_part(kn))
-
-        @pl.when(has_next & (kn >= 0) & (kn < NC))
+        @pl.when((k >= 0) & (2 * k + 4 < NC))
+        def _():
+            queries(2 * k + 4, False)
+
+        @pl.when(has_prev & (k == 1))
+        def _():
+            lift()
+
+        @pl.when(nearby & jnp.logical_not(full))
+        def _():
+            by_parity(lambda even: unit(near_part(kn, even)))
+
+        @pl.when(nearby)
         def _():
             send_near(kn)
 
-        @pl.when((k >= 1) & (lax.rem(k, 2) == 1) & (k + 3 < NC))
-        def _():
-            queries(k + 3, False)
-
-        @pl.when((k >= G + 2) & (lax.rem(k - 2, G) == 0))
-        def _():
-            finish((k - G - 2) // G)
-
-        @pl.when((k >= G + 4) & (lax.rem(k - 4, G) == 0))
-        def _():
-            middle((k - G - 4) // G)
-
-        @pl.when((k >= 2 * G + 4) & (lax.rem(k - 4, G) == 0))
-        def _():
-            close((k - 2 * G - 4) // G)
+        @pl.when(middling & jnp.logical_not(full))
+        def _():
+            by_parity(lambda even: unit(own_part(k - 1, even)))
+
+        @pl.when(k == 3)
+        def _():
+            finish(0, 1)
+
+        paired = (lax.rem(k, 2) == 1) & (k <= NC + 1)
+
+        @pl.when(paired & (k >= 5))
+        def _():
+            finish(k - 4, 2)
+
+        @pl.when(k == NC + 2)
+        def _():
+            finish(NC - 1, 1)
+
+        @pl.when(k == 4)
+        def _():
+            middle(0, 1)
+
+        @pl.when(paired & (k >= 7))
+        def _():
+            middle(k - 6, 2)
+
+        @pl.when(k == 6)
+        def _():
+            close(0, 1)
+
+        @pl.when(paired & (k >= 9))
+        def _():
+            close(k - 8, 2)
 
         return carry
 
     lax.fori_loop(-1, NC + 3, step, 0)
-    rest = [(G * f + 2 * G + 4, 0, f) for f in range(NF)] + [(G * f + G + 4, 1, f) for f in range(NF)]
-    for at, kind, f in sorted(rest):
-        if at >= NC + 3:
-            (close, middle)[kind](f)
+    middle(NC - 3, 2)
+    if NC > 4:
+        close(NC - 5, 2)
+    middle(NC - 1, 1)
+    close(NC - 3, 2)
+    close(NC - 1, 1)
+
+    @pl.when(has_next)
+    def _():
+        for h in range(UP):
+            for cp in kv_up(h):
+                cp.wait_send()
+
+    @pl.when(has_prev & (odd == 1))
+    def _():
+        for h in range(UP):
+            for cp in kv_across(h):
+                cp.wait_send()
 
     def drain(h, carry):
         for cp in kv_partner(h):
@@ -535,13 +641,22 @@
 
     lax.fori_loop(0, NC, drain_chunks, 0)
 
+    def drain_phases(c, count):
+        for cp in first_phase(c, count) + second_phase(c, count):
+            cp.wait_send()
+
+    def drain_pairs(g, carry):
+        drain_phases(2 * g + 1, 2)
+        return carry
+
     def drain_out(c, carry):
-        for cp in first_phase(c) + second_phase(c):
-            cp.wait_send()
         out_copy(c).wait()
         return carry
 
-    lax.fori_loop(0, NF, drain_out, 0)
+    drain_phases(0, 1)
+    lax.fori_loop(0, NC // 2 - 1, drain_pairs, 0)
+    drain_phases(NC - 1, 1)
+    lax.fori_loop(0, NC, drain_out, 0)
 
 
 def shards(n, n_tp, hidden_in, pre_gain, w_query, key_cache, value_cache, w_out, post_gain, starts, counts):
@@ -550,7 +665,6 @@
     kvh = kvw // HD
     sub = SUB
     NC = rows // (n_tp * sub)
-    NF = NC // G
     chunk = rows // NC
     tall = 2 * chunk
     nx, ny, half = 2, n_tp // 2, d // 2
@@ -572,6 +686,9 @@
             kv,
             pltpu.VMEM((2, kvh, HD, ctx), BF16),
             kv,
+            pltpu.VMEM((2, UP, ctx, HD), BF16),
+            pltpu.VMEM((2, UP, HD, ctx), BF16),
+            pltpu.VMEM((2, UP, ctx, HD), BF16),
             queries, queries, queries,
             partial, partial, partial, partial,
             pltpu.VMEM((NC, kvh, tall, HD), F32),
@@ -585,22 +702,23 @@
             pltpu.VMEM((tall, KT), BF16), pltpu.VMEM((tall, KT), BF16),
             pltpu.VMEM((2 * n_tp, sub, HD), F32),
             pltpu.VMEM((1, d), F32), pltpu.VMEM((1, d), F32),
-            pltpu.VMEM((NF, ny, nx, G, sub, d), BF16),
-            pltpu.VMEM((NF, nx - 1, ny, G, sub, half), BF16),
-            pltpu.VMEM((NF, ny, G, sub, half), BF16),
-            pltpu.VMEM((NF, ny - 1, G, sub, half), BF16),
-            pltpu.VMEM((NF, ny - 1, nx, G, sub, half), BF16),
-            pltpu.VMEM((NF, nx, G, sub, half), BF16),
-            pltpu.VMEM((NF, nx - 1, G, sub, half), BF16),
+            pltpu.VMEM((NC, ny, nx, sub, d), BF16),
+            pltpu.VMEM((nx - 1, NC, ny, sub, half), BF16),
+            pltpu.VMEM((NC, ny, sub, half), BF16),
+            pltpu.VMEM((ny - 1, NC, sub, half), BF16),
+            pltpu.VMEM((ny - 1, NC, nx, sub, half), BF16),
+            pltpu.VMEM((NC, nx, sub, half), BF16),
+            pltpu.VMEM((nx - 1, NC, sub, half), BF16),
             pltpu.VMEM((rows // n_tp, d), BF16),
-            pltpu.VMEM((NF, G * sub, d), BF16),
-            pltpu.VMEM((G * chunk, w_out.shape[0]), BF16),
-            dma((NC, n_tp)), dma((kvh,)), dma, dma((kvh, 2)), dma, dma((NF,)), dma((2,)),
+            pltpu.VMEM((NC, sub, d), BF16),
+            pltpu.VMEM((2 * chunk, w_out.shape[0]), BF16),
+            dma((NC, n_tp)), dma((kvh,)), dma, dma((kvh, 2)), dma, dma((NC,)), dma((2,)),
             dma((kvh, 2)), dma((kvh, 2)),
+            dma((UP, 2)), dma((UP, 2)), dma((UP, 2)), dma((UP, 2)),
             dma((NC,)), dma((NC,)), dma((NC,)), dma((NC,)),
             dma((NC,)), dma((NC,)), dma((NC,)), dma((NC,)),
-            dma((NF, nx - 1)), dma((NF, nx - 1)), dma((NF, ny - 1)), dma((NF, ny - 1)),
-            dma((NF, ny - 1)), dma((NF, ny - 1)), dma((NF, nx - 1)), dma((NF, nx - 1)),
+            dma((NC, nx - 1)), dma((NC, nx - 1)), dma((NC, ny - 1)), dma((NC, ny - 1)),
+            dma((NC, ny - 1)), dma((NC, ny - 1)), dma((NC, nx - 1)), dma((NC, nx - 1)),
         ],
         compiler_params=pltpu.CompilerParams(
             collective_id=0, has_side_effects=True, vmem_limit_bytes=67_000_000),

time: 94.8 us -> 90.4 us (0.954)
  Pallas kernels: 92.3 us -> 87.9 us
    pallas_call x1, Pallas kernels: 92.3 us -> 87.9 us  [shards(): pl.pallas_call(functools.partial(kernel, n, n_tp, kvh, NC), out_shape=jax...]
where the time goes in v3:
time: 90.4 us; the launch traced here: 90.2 us
  Pallas kernels  87.9 us (97%)
  local copies, waits for them, and re-layouts  2.36 us (3%)
    pallas_call x1, Pallas kernels, shards(): pl.pallas_call(functools.partial(kernel, n, n_tp, kvh, NC), out_shape=jax...  87.9 us
    unnamed x1, local copies, waits for them, and re-layouts  2.36 us

profile of v3, /device:TPU:0, one launch (start us, length us, event | category | flops | bytes accessed | tf_op | source)
XLA Modules:
  0.0 90.2 jit_solution(10453793273075148010)
XLA Ops:
  0.0 87.9 %attention_block.1 = bf16[128,4608]{1,0:T(8,128)(2,1)} custom-call(s32[8]{0:T(128)} %starts.1, s32[8]{0:T(128)} %counts.1, bf16[512,4608]{1,0:T(8,128)(2,1)} %hidden.1, f32[4608]{0:T(1024)} %gain_in.1, bf16[4608,1024]{1,0:T(8,128)(2,1)} %wq.1, bf16[1024,512]{1,0:T(8,128)(2,1)} %key.1, bf16[1024,512]{1,0:T(8,128)(2,1)} %value.1, bf16[1024,4608]{1,0:T(8,128)(2,1)} %wout.1, ...), custom_call_target="tpu_custom_call" | custom-call | tf_op jit(solution)/shard_map/attention_block/pallas_call | solution.py:677
  87.9 2.4 %copy.11 = bf16[128,4608]{1,0:T(8,128)(2,1)} copy(bf16[128,4608]{1,0:T(8,128)(2,1)} %attention_block.1) | data formatting | bytes 2359296

commit v4 on v3

--- a/solution.py
+++ b/solution.py
@@ -553,13 +553,13 @@
         def _():
             by_parity(lambda even: unit(near_part(kn, even)))
 
+        @pl.when(middling & jnp.logical_not(full))
+        def _():
+            by_parity(lambda even: unit(own_part(k - 1, even)))
+
         @pl.when(nearby)
         def _():
             send_near(kn)
-
-        @pl.when(middling & jnp.logical_not(full))
-        def _():
-            by_parity(lambda even: unit(own_part(k - 1, even)))
 
         @pl.when(k == 3)
         def _():

time: 90.4 us -> 90.4 us (level)
  no operation moved by 1% of the time
where the time goes in v4:
time: 90.4 us; the launch traced here: 90.2 us
  Pallas kernels  87.9 us (97%)
  local copies, waits for them, and re-layouts  2.36 us (3%)
    pallas_call x1, Pallas kernels, shards(): pl.pallas_call(functools.partial(kernel, n, n_tp, kvh, NC), out_shape=jax...  87.9 us
    unnamed x1, local copies, waits for them, and re-layouts  2.36 us

profile of v4, /device:TPU:0, one launch (start us, length us, event | category | flops | bytes accessed | tf_op | source)
XLA Modules:
  0.0 90.2 jit_solution(10195480568196471004)
XLA Ops:
  0.0 87.9 %attention_block.1 = bf16[128,4608]{1,0:T(8,128)(2,1)} custom-call(s32[8]{0:T(128)} %starts.1, s32[8]{0:T(128)} %counts.1, bf16[512,4608]{1,0:T(8,128)(2,1)} %hidden.1, f32[4608]{0:T(1024)} %gain_in.1, bf16[4608,1024]{1,0:T(8,128)(2,1)} %wq.1, bf16[1024,512]{1,0:T(8,128)(2,1)} %key.1, bf16[1024,512]{1,0:T(8,128)(2,1)} %value.1, bf16[1024,4608]{1,0:T(8,128)(2,1)} %wout.1, ...), custom_call_target="tpu_custom_call" | custom-call | tf_op jit(solution)/shard_map/attention_block/pallas_call | solution.py:677
  87.9 2.4 %copy.11 = bf16[128,4608]{1,0:T(8,128)(2,1)} copy(bf16[128,4608]{1,0:T(8,128)(2,1)} %attention_block.1) | data formatting | bytes 2359296
